TPU v7x, 32 devices: a whole 2x2x4 slice. The times are simulated.
32 devices in a mesh: expert: 4 (over y, core), shard: 8 (over z, x).
Axes of the slice: x: 2, y: 2, z: 4, core: 2. Of those that a mesh axis runs over, the one named last changes fastest.
Arguments:
- master_gate: float32 [128, 2048, 768], P('expert', 'shard'), may hold values from -0.125 to 0.125
- second_gate: bfloat16 [128, 2048, 768], P('expert', 'shard'), may hold values from -0.0625 to 0.0625
- master_up: float32 [128, 2048, 768], P('expert', 'shard'), may hold values from -0.125 to 0.125
- second_up: bfloat16 [128, 2048, 768], P('expert', 'shard'), may hold values from -0.0625 to 0.0625
- router_weight: float32 [2048, 128], P('shard', 'expert'), may hold values from -0.125 to 0.125
- router_gain: float32 [2048], P('shard'), may hold values from 0.25 to 1.75
Outputs:
- final_gate: bfloat16 [128, 768, 2048], P('expert', 'shard')
- final_up: bfloat16 [128, 768, 2048], P('expert', 'shard')
- serve_router: bfloat16 [2048, 128], replicated
All inputs are finite; a program needn't handle non-finite values.
Results may differ from a plain program's by a relative error of at most 0.001.
Values may be sent and summed in bfloat16 or wider, within the bound.
A program may use at most 192 MiB of HBM per device.

v0:
```python
import jax
import jax.numpy as jnp
from jax import lax
from jax.sharding import PartitionSpec as P


def shards(master_gate, second_gate, master_up, second_up, router_weight, router_gain):
    merged_gate = master_gate + second_gate.astype(jnp.float32)
    merged_up = master_up + second_up.astype(jnp.float32)
    narrow_gate, narrow_up = (merged_gate.astype(jnp.bfloat16), merged_up.astype(jnp.bfloat16))
    final_gate, final_up = (
        lax.all_to_all(narrow_gate, "shard", split_axis=2, concat_axis=1, tiled=True),
        lax.all_to_all(narrow_up, "shard", split_axis=2, concat_axis=1, tiled=True),
    )
    final_gate = jnp.transpose(final_gate, (0, 2, 1))
    final_up = jnp.transpose(final_up, (0, 2, 1))
    part_router = (router_weight * router_gain[:, None]).astype(jnp.bfloat16)
    row_router = lax.all_gather(part_router, "shard", axis=0, tiled=True)
    serve_router = lax.all_gather(row_router, "expert", axis=1, tiled=True)
    return (final_gate, final_up, serve_router)


def solution(mesh):
    in_specs = (
        P("expert", "shard", None),
        P("expert", "shard", None),
        P("expert", "shard", None),
        P("expert", "shard", None),
        P("shard", "expert"),
        P("shard"),
    )
    out_specs = (P("expert", "shard", None), P("expert", "shard", None), P())
    return jax.shard_map(shards, mesh=mesh, in_specs=in_specs, out_specs=out_specs, check_vma=False)
```

profile of v0, /device:TPU:0, one launch (start us, length us, event | category | flops | bytes accessed | tf_op | source)
XLA Modules:
  0.0 713.1 jit_solution(3689968632232905963)
XLA Ops:
  0.6 25.0 %copy.25 = f32[32,256,768]{1,0,2:T(8,128)} copy(f32[32,256,768]{2,1,0:T(8,128)} %param.6) | data formatting | bytes 50331648 | tf_op args[0]
  25.7 16.9 %copy.24 = bf16[32,256,768]{1,0,2:T(8,128)(2,1)} copy(bf16[32,256,768]{2,1,0:T(8,128)(2,1)} %param.7) | data formatting | bytes 25165824 | tf_op args[1]
  42.5 17.3 %add_convert_fusion.1 = bf16[32,256,768]{1,0,2:T(8,128)(2,1)} fusion(f32[32,256,768]{1,0,2:T(8,128)} %copy.25, bf16[32,256,768]{1,0,2:T(8,128)(2,1)} %copy.24), kind=kLoop, calls=%fused_computation.1 | loop fusion | flops 18874368 | bytes 50331648 | tf_op jit(solution)/shard_map/convert_element_type | solution.py:10
  59.8 7.3 %all-to-all-start = ((bf16[32,256,768]{1,0,2:T(8,128)(2,1)}), bf16[32,256,768]{1,0,2:T(8,128)(2,1)}, u32[]{:S(2)}, u32[]{:S(2)}) async-start(bf16[32,256,768]{1,0,2:T(8,128)(2,1)} %add_convert_fusion.1), calls=%async_computation | async-start | bytes 25165824 | tf_op jit(solution)/shard_map/all_to_all | solution.py:12
  67.1 25.0 %copy.29 = f32[32,256,768]{1,0,2:T(8,128)} copy(f32[32,256,768]{2,1,0:T(8,128)} %param.8) | data formatting | bytes 50331648 | tf_op args[2]
  92.2 16.9 %copy.28 = bf16[32,256,768]{1,0,2:T(8,128)(2,1)} copy(bf16[32,256,768]{2,1,0:T(8,128)(2,1)} %param.9) | data formatting | bytes 25165824 | tf_op args[3]
  109.0 17.3 %add_convert_fusion = bf16[32,256,768]{1,0,2:T(8,128)(2,1)} fusion(f32[32,256,768]{1,0,2:T(8,128)} %copy.29, bf16[32,256,768]{1,0,2:T(8,128)(2,1)} %copy.28), kind=kLoop, calls=%fused_computation | loop fusion | flops 18874368 | bytes 50331648 | tf_op jit(solution)/shard_map/convert_element_type | solution.py:10
  126.3 0.0 copy-start
  126.3 0.0 copy-start.1
  126.3 213.9 %all-to-all-done = bf16[32,256,768]{1,0,2:T(8,128)(2,1)} async-done(((bf16[32,256,768]{1,0,2:T(8,128)(2,1)}), bf16[32,256,768]{1,0,2:T(8,128)(2,1)}, u32[]{:S(2)}, u32[]{:S(2)}) %all-to-all-start) | async-done | bytes 12582944 | tf_op jit(solution)/shard_map/all_to_all | solution.py:12
  340.2 5.3 all-to-all-start.1
  345.5 0.0 copy-done
  345.5 0.0 copy-done.1
  345.6 292.2 %all_gather.6 = bf16[2048,32]{0,1:T(8,128)(2,1)S(1)} all-gather(bf16[256,32]{0,1:T(8,128)(2,1)S(1)} %multiply_convert_fusion), channel_id=1, replica_groups=mesh['expert'=4,'shard'=8] {'shard'}, dimensions={0}, use_global_device_ids=true | all-gather | bytes 147456 | tf_op jit(solution)/shard_map/all_gather | solution.py:18
  637.8 7.2 %all_gather.7 = bf16[2048,128]{0,1:T(8,128)(2,1)S(1)} all-gather(bf16[2048,32]{0,1:T(8,128)(2,1)S(1)} %all_gather.6), channel_id=1, replica_groups=mesh['expert'=4,'shard'=8] {'expert'}, dimensions={1}, use_global_device_ids=true | all-gather | bytes 655360 | tf_op jit(solution)/shard_map/all_gather | solution.py:19
  645.0 1.0 copy.32
  646.0 14.1 %copy.27 = bf16[32,8,256,96]{2,1,3,0:T(8,128)(2,1)} copy(bf16[32,8,256,96]{2,0,3,1:T(8,128)(2,1)} %bitcast.2) | data formatting | bytes 25165824 | tf_op jit(solution)/shard_map/all_to_all | solution.py:12
  660.0 19.5 %all_to_all.29 = bf16[32,2048,96]{1,2,0:T(8,128)(2,1)} reshape(bf16[32,8,256,96]{2,1,3,0:T(8,128)(2,1)} %copy.27) | data formatting | bytes 25165824 | tf_op jit(solution)/shard_map/all_to_all | solution.py:12
  679.5 0.0 all-to-all-done.1
  679.5 14.1 %copy.31 = bf16[32,8,256,96]{2,1,3,0:T(8,128)(2,1)} copy(bf16[32,8,256,96]{2,0,3,1:T(8,128)(2,1)} %bitcast.6) | data formatting | bytes 25165824 | tf_op jit(solution)/shard_map/all_to_all | solution.py:13
  693.6 19.5 %all_to_all.33 = bf16[32,2048,96]{1,2,0:T(8,128)(2,1)} reshape(bf16[32,8,256,96]{2,1,3,0:T(8,128)(2,1)} %copy.31) | data formatting | bytes 25165824 | tf_op jit(solution)/shard_map/all_to_all | solution.py:13
  (1 shorter events, 0.0 us)
Async XLA Ops:
  59.8 280.3 %all-to-all-start = ((bf16[32,256,768]{1,0,2:T(8,128)(2,1)}), bf16[32,256,768]{1,0,2:T(8,128)(2,1)}, u32[]{:S(2)}, u32[]{:S(2)}) async-start(bf16[32,256,768]{1,0,2:T(8,128)(2,1)} %add_convert_fusion.1), calls=%async_computation | async-start | bytes 25165824 | tf_op jit(solution)/shard_map/all_to_all | solution.py:12
  126.3 219.2 %copy-start = (f32[256,32]{0,1:T(8,128)S(1)}, f32[256,32]{0,1:T(8,128)}, u32[]{:S(2)}) copy-start(f32[256,32]{0,1:T(8,128)} %param.10) | copy-start | bytes 98308
  126.3 219.2 %copy-start.1 = (f32[256]{0:T(256)S(1)}, f32[256]{0:T(256)}, u32[]{:S(2)}) copy-start(f32[256]{0:T(256)} %param.11) | copy-start | bytes 3076
  340.2 339.3 %all-to-all-start.1 = ((bf16[32,256,768]{1,0,2:T(8,128)(2,1)}), bf16[32,256,768]{1,0,2:T(8,128)(2,1)}, u32[]{:S(2)}, u32[]{:S(2)}) async-start(bf16[32,256,768]{1,0,2:T(8,128)(2,1)} %add_convert_fusion), calls=%async_computation.1 | async-start | bytes 25165824 | tf_op jit(solution)/shard_map/all_to_all | solution.py:13
where the time goes:
time: 716 us; the launch traced here: 713 us
  blocking collectives  299 us (42%)
  waiting for transfers between devices  214 us (30%)
  local copies, waits for them, and re-layouts  152 us (21%)
  other arithmetic  34.6 us (5%)
  starting transfers between devices  12.6 us (2%)
    all_gather x1, blocking collectives, shards(): row_router = lax.all_gather(part_router, 'shard', axis=0, tiled=True)  292 us
    all_to_all x1, waiting for transfers between devices, shards(): lax.all_to_all(narrow_gate, 'shard', split_axis=2, concat_axis=1, tiled=T...  214 us
    unnamed x9, local copies, waits for them, and re-layouts  84.8 us
    all_to_all x2, local copies, waits for them, and re-layouts, shards(): lax.all_to_all(narrow_up, 'shard', split_axis=2, concat_axis=1, tiled=True)  33.6 us
    all_to_all x2, local copies, waits for them, and re-layouts, shards(): lax.all_to_all(narrow_gate, 'shard', split_axis=2, concat_axis=1, tiled=T...  33.5 us
    convert_element_type x1, other arithmetic, shards(): merged_gate.astype(jnp.bfloat16)  17.3 us
    convert_element_type x1, other arithmetic, shards(): merged_up.astype(jnp.bfloat16)  17.3 us
  transfers between devices with their start and end apart: 2, of which 1 were waited for; matrix products, arithmetic and copies ran while one was open for 10% of the time, Pallas kernels for 0%

commit v1 on v0

--- a/solution.py
+++ b/solution.py
@@ -1,10 +1,18 @@
+import functools
+
 import jax
 import jax.numpy as jnp
 from jax import lax
+from jax.experimental import pallas as pl
+from jax.experimental.pallas import tpu as pltpu
 from jax.sharding import PartitionSpec as P
 
-
-def shards(master_gate, second_gate, master_up, second_up, router_weight, router_gain):
+SLOTS = 12
+LOADS = 2
+MESH_IDS = pl.DeviceIdType.MESH
+
+
+def plain(master_gate, second_gate, master_up, second_up, router_weight, router_gain):
     merged_gate = master_gate + second_gate.astype(jnp.float32)
     merged_up = master_up + second_up.astype(jnp.float32)
     narrow_gate, narrow_up = (merged_gate.astype(jnp.bfloat16), merged_up.astype(jnp.bfloat16))
@@ -20,7 +28,225 @@
     return (final_gate, final_up, serve_router)
 
 
+def peers(me, n):
+    half = n // 2
+    mine, place = me // half, me % half
+    far = [(1 - mine) * half + (place + i) % half for i in range(half)]
+    near = [mine * half + (place + i) % half for i in range(1, half)]
+    return far + near
+
+
+def regroup_kernel(n, groups, mg, sg, mu, su, rw, gain, og, ou, orr,
+                   in_m, in_s, stage, rw_v, gain_v, r_part, r_all,
+                   load_m, load_s, load_r, send, own, recv, r_send, r_recv, f_send, f_recv):
+    experts, rows, inner = mg.shape
+    part = inner // n
+    r_cols = rw.shape[0]
+    group, me = lax.axis_index("expert"), lax.axis_index("shard")
+    to = peers(me, n)
+    other = [(group + i) % groups for i in range(1, groups)]
+    masters, seconds, outs = (mg, mu), (sg, su), (og, ou)
+    home = pl.ds(pl.multiple_of(me * rows, rows), rows)
+
+    def loads(a, e):
+        slot = e % LOADS
+        return (
+            pltpu.make_async_copy(masters[a].at[e], in_m.at[a, slot], load_m.at[a, slot]),
+            pltpu.make_async_copy(seconds[a].at[e], in_s.at[a, slot], load_s.at[a, slot]),
+        )
+
+    def start_loads(a, e):
+        for copy in loads(a, e):
+            copy.start()
+
+    def router_loads():
+        return (
+            pltpu.make_async_copy(rw, rw_v, load_r.at[0]),
+            pltpu.make_async_copy(gain, gain_v, load_r.at[1]),
+        )
+
+    def block(a, e, device):
+        src = pl.ds(pl.multiple_of(device * part, part), part)
+        return stage.at[a, e % SLOTS, src, :], outs[a].at[e, :, home]
+
+    def start_sends(a, e):
+        for device in to:
+            src, dst = block(a, e, device)
+            pltpu.make_async_remote_copy(
+                src_ref=src, dst_ref=dst, send_sem=send.at[a, e % SLOTS], recv_sem=recv.at[a, e],
+                device_id=(group, device), device_id_type=MESH_IDS,
+            ).start()
+        src, dst = block(a, e, me)
+        pltpu.make_async_copy(src, dst, own.at[a, e % SLOTS]).start()
+
+    def wait_sends(a, e):
+        many = stage.at[a, e % SLOTS, pl.ds(0, (n - 1) * part), :]
+        pltpu.make_async_copy(many, many, send.at[a, e % SLOTS]).wait()
+        src, dst = block(a, e, me)
+        pltpu.make_async_copy(src, dst, own.at[a, e % SLOTS]).wait()
+
+    def merge(a, e):
+        for copy in loads(a, e):
+            copy.wait()
+
+        @pl.when(e >= SLOTS)
+        def _():
+            wait_sends(a, e - SLOTS)
+
+        slot, into = e % LOADS, e % SLOTS
+        for c in range(inner // 128):
+            cols = slice(c * 128, (c + 1) * 128)
+            merged = in_m[a, slot, :, cols] + in_s[a, slot, :, cols].astype(jnp.float32)
+            stage[a, into, cols, :] = merged.T.astype(jnp.bfloat16)
+
+        @pl.when(e + LOADS < experts)
+        def _():
+            start_loads(a, e + LOADS)
+
+    for a in range(2):
+        start_loads(a, 0)
+    for copy in router_loads():
+        copy.start()
+    for e in range(1, LOADS):
+        for a in range(2):
+            start_loads(a, e)
+
+    barrier = pltpu.get_barrier_semaphore()
+    for device in to:
+        pl.semaphore_signal(barrier, inc=1, device_id=(group, device), device_id_type=MESH_IDS)
+    for g in other:
+        pl.semaphore_signal(barrier, inc=1, device_id=(g, me), device_id_type=MESH_IDS)
+
+    merge(0, 0)
+    for copy in router_loads():
+        copy.wait()
+    mine = (rw_v[...] * gain_v[...]).astype(jnp.bfloat16)
+    r_rows = pl.ds(pl.multiple_of(group * r_cols, r_cols), r_cols)
+    r_part[...] = mine
+    r_all[r_rows, home] = mine
+    pl.semaphore_wait(barrier, len(to) + len(other))
+
+    def after_first(e):
+        merge(1, e)
+        start_sends(0, e)
+
+    after_first(0)
+    for device in to:
+        pltpu.make_async_remote_copy(
+            src_ref=r_part, dst_ref=r_all.at[r_rows, home], send_sem=r_send, recv_sem=r_recv,
+            device_id=(group, device), device_id_type=MESH_IDS,
+        ).start()
+
+    def step(e, carry):
+        merge(0, e)
+        start_sends(1, e - 1)
+        after_first(e)
+        return carry
+
+    lax.fori_loop(1, experts, step, 0)
+
+    many = r_all.at[pl.ds(0, r_cols), pl.ds(0, (n - 1) * rows)]
+    pltpu.make_async_copy(many, many, r_recv).wait()
+    pltpu.make_async_copy(many, many, r_send).wait()
+    start_sends(1, experts - 1)
+    for g in other:
+        pltpu.make_async_remote_copy(
+            src_ref=r_all.at[r_rows, :], dst_ref=r_all.at[r_rows, :], send_sem=f_send, recv_sem=f_recv,
+            device_id=(g, me), device_id_type=MESH_IDS,
+        ).start()
+    many = r_all.at[pl.ds(0, (groups - 1) * r_cols), :]
+    pltpu.make_async_copy(many, many, f_recv).wait()
+    pltpu.make_async_copy(many, many, f_send).wait()
+    for c in range(orr.shape[0] // 128):
+        span = slice(c * 128, (c + 1) * 128)
+        orr[span, :] = r_all[:, span].astype(jnp.float32).T.astype(jnp.bfloat16)
+
+    def drain(e, carry):
+        for a in range(2):
+            wait_sends(a, e)
+        return carry
+
+    lax.fori_loop(max(experts - SLOTS, 0), experts, drain, 0)
+
+    def arrive(e, carry):
+        for a in range(2):
+            many = outs[a].at[e, :, pl.ds(0, (n - 1) * rows)]
+            pltpu.make_async_copy(many, many, recv.at[a, e]).wait()
+        return carry
+
+    lax.fori_loop(0, experts, arrive, 0)
+
+
+def put_kernel(gate, up, router, og, ou, orr, done):
+    copies = [
+        pltpu.make_async_copy(src, dst, done.at[i])
+        for i, (src, dst) in enumerate(((gate, og), (up, ou), (router, orr)))
+    ]
+    for copy in copies:
+        copy.start()
+    for copy in copies:
+        copy.wait()
+
+
+def put(*held):
+    anywhere = pl.BlockSpec(memory_space=pl.ANY)
+    return pl.pallas_call(
+        put_kernel,
+        out_shape=tuple(pltpu.HBM(x.shape, x.dtype) for x in held),
+        in_specs=[anywhere] * len(held),
+        out_specs=(anywhere,) * len(held),
+        scratch_shapes=[pltpu.SemaphoreType.DMA((len(held),))],
+        compiler_params=pltpu.CompilerParams(vmem_limit_bytes=1024 * 1024),
+        name="put",
+    )(*held)
+
+
+def fused(n, groups, master_gate, second_gate, master_up, second_up, router_weight, router_gain):
+    experts, rows, inner = master_gate.shape
+    r_cols = router_weight.shape[1]
+    final = (experts, inner // n, rows * n)
+    anywhere = pl.BlockSpec(memory_space=pl.ANY)
+    dma = pltpu.SemaphoreType.DMA
+    return put(*pl.pallas_call(
+        functools.partial(regroup_kernel, n, groups),
+        out_shape=(
+            pltpu.VMEM(final, jnp.bfloat16),
+            pltpu.VMEM(final, jnp.bfloat16),
+            jax.ShapeDtypeStruct((rows * n, r_cols * groups), jnp.bfloat16),
+        ),
+        in_specs=[anywhere] * 6,
+        out_specs=(anywhere, anywhere, pl.BlockSpec(memory_space=pltpu.VMEM)),
+        scratch_shapes=[
+            pltpu.VMEM((2, LOADS, rows, inner), jnp.float32),
+            pltpu.VMEM((2, LOADS, rows, inner), jnp.bfloat16),
+            pltpu.VMEM((2, SLOTS, inner, rows), jnp.bfloat16),
+            pltpu.VMEM((r_cols, rows), jnp.float32),
+            pltpu.VMEM((1, rows), jnp.float32),
+            pltpu.VMEM((r_cols, rows), jnp.bfloat16),
+            pltpu.VMEM((r_cols * groups, rows * n), jnp.bfloat16),
+            dma((2, LOADS)), dma((2, LOADS)), dma((2,)),
+            dma((2, SLOTS)), dma((2, SLOTS)), dma((2, experts)),
+            dma, dma, dma, dma,
+        ],
+        compiler_params=pltpu.CompilerParams(
+            collective_id=0, has_side_effects=True, vmem_limit_bytes=24 * 1024 * 1024,
+        ),
+        name="regroup",
+    )(master_gate, second_gate, master_up, second_up, router_weight.T, router_gain[None, :]))
+
+
 def solution(mesh):
+    n, groups = mesh.shape["shard"], mesh.shape["expert"]
+
+    def shards(*args):
+        experts, rows, inner = args[0].shape
+        r_cols = args[4].shape[1]
+        fits = (
+            n % 2 == 0 and groups > 1 and rows % 128 == 0 and inner % 128 == 0
+            and (inner // n) % 16 == 0 and r_cols % 16 == 0 and experts >= max(SLOTS, LOADS)
+        )
+        return fused(n, groups, *args) if fits else plain(*args)
+
     in_specs = (
         P("expert", "shard", None),
         P("expert", "shard", None),

time: 716 us -> 562 us (0.78)
  Pallas kernels: 0 us -> 560 us
  blocking collectives: 299 us -> 0 us
  waiting for transfers between devices: 214 us -> 0 us
  local copies, waits for them, and re-layouts: 152 us -> 1.43 us
  other arithmetic: 34.6 us -> 0 us
  starting transfers between devices: 12.6 us -> 0 us
    pallas_call x0 -> x2, Pallas kernels: none -> 560 us  [the longest x1 551 us: fused(): pl.pallas_call(functools.partial(regroup_kernel, n, groups), out_shape=(p...]
    all_gather x2 -> x0, blocking collectives: 299 us -> none  [the longest x1 292 us: shards(): row_router = lax.all_gather(part_router, 'shard', axis=0, tiled=True)]
    all_to_all x2 -> x0, waiting for transfers between devices: 214 us -> none  [the longest x1 214 us: shards(): lax.all_to_all(narrow_gate, 'shard', split_axis=2, concat_axis=1, tiled=T...]
    unnamed x9 -> x4, local copies, waits for them, and re-layouts: 84.8 us -> 1.43 us
    all_to_all x4 -> x0, local copies, waits for them, and re-layouts: 67.1 us -> none  [the longest x2 33.6 us: shards(): lax.all_to_all(narrow_up, 'shard', split_axis=2, concat_axis=1, tiled=True)]
    convert_element_type x3 -> x0, other arithmetic: 34.6 us -> none  [the longest x1 17.3 us: shards(): merged_gate.astype(jnp.bfloat16)]
    all_to_all x2 -> x0, starting transfers between devices: 12.6 us -> none  [the longest x1 7.28 us: shards(): lax.all_to_all(narrow_gate, 'shard', split_axis=2, concat_axis=1, tiled=T...]
  transfers between devices with their start and end apart: 2 -> 0, of which waited for: 1 -> 0; matrix products, arithmetic and copies ran while one was open for 10% -> 0% of each run, Pallas kernels for 0% -> 0%
where the time goes in v1:
time: 562 us
  Pallas kernels  560 us (100%)
    pallas_call x1, Pallas kernels, fused(): pl.pallas_call(functools.partial(regroup_kernel, n, groups), out_shape=(p...  551 us

profile of v1, /device:TPU:0, one launch (start us, length us, event | category | flops | bytes accessed | tf_op | source)
XLA Modules:
  0.0 562.1 jit_solution(14633553778768735223)
XLA Ops:
  0.6 0.0 copy-start
  0.6 0.7 copy-done
  1.4 0.0 copy-start.1
  1.4 0.7 copy-done.1
  2.1 551.0 %regroup.1 = (bf16[32,96,2048]{2,1,0:T(8,128)(2,1)S(1)}, bf16[32,96,2048]{2,1,0:T(8,128)(2,1)S(1)}, bf16[2048,128]{1,0:T(8,128)(2,1)S(1)}) custom-call(f32[32,256,768]{2,1,0:T(8,128)} %mg.1, bf16[32,256,768]{2,1,0:T(8,128)(2,1)} %sg.1, f32[32,256,768]{2,1,0:T(8,128)} %mu.1, bf16[32,256,768]{2,1,0:T(8,128)(2,1)} %su.1, f32[32,256]{1,0:T(8,128)S(1)} %bitcast.2, ...), custom_call_target="tpu_custom_call" | custom-call | tf_op jit(solution)/shard_map/regroup/pallas_call | solution.py:210
  553.1 8.9 %put.1 = (bf16[32,96,2048]{2,1,0:T(8,128)(2,1)}, bf16[32,96,2048]{2,1,0:T(8,128)(2,1)}, bf16[2048,128]{1,0:T(8,128)(2,1)}) custom-call(bf16[32,96,2048]{2,1,0:T(8,128)(2,1)S(1)} %get-tuple-element.6.gate, bf16[32,96,2048]{2,1,0:T(8,128)(2,1)S(1)} %get-tuple-element.7.up, bf16[2048,128]{1,0:T(8,128)(2,1)S(1)} %get-tuple-element.8.router), custom_call_target="tpu_custom_call" | custom-call | tf_op jit(solution)/shard_map/put/pallas_call | solution.py:193
Async XLA Ops:
  0.6 0.8 copy-start
  1.4 0.7 copy-start.1

commit v2 on v1

--- a/solution.py
+++ b/solution.py
@@ -33,7 +33,7 @@
     mine, place = me // half, me % half
     far = [(1 - mine) * half + (place + i) % half for i in range(half)]
     near = [mine * half + (place + i) % half for i in range(1, half)]
-    return far + near
+    return far, near
 
 
 def regroup_kernel(n, groups, mg, sg, mu, su, rw, gain, og, ou, orr,
@@ -43,7 +43,8 @@
     part = inner // n
     r_cols = rw.shape[0]
     group, me = lax.axis_index("expert"), lax.axis_index("shard")
-    to = peers(me, n)
+    far, near = peers(me, n)
+    to = far + near
     other = [(group + i) % groups for i in range(1, groups)]
     masters, seconds, outs = (mg, mu), (sg, su), (og, ou)
     home = pl.ds(pl.multiple_of(me * rows, rows), rows)
@@ -125,30 +126,41 @@
     r_part[...] = mine
     r_all[r_rows, home] = mine
     pl.semaphore_wait(barrier, len(to) + len(other))
-
-    def after_first(e):
-        merge(1, e)
-        start_sends(0, e)
-
-    after_first(0)
-    for device in to:
+    start_sends(0, 0)
+    merge(1, 0)
+
+    def hand(src, dst, i, device):
         pltpu.make_async_remote_copy(
-            src_ref=r_part, dst_ref=r_all.at[r_rows, home], send_sem=r_send, recv_sem=r_recv,
+            src_ref=src, dst_ref=dst, send_sem=r_send.at[i], recv_sem=r_recv.at[i],
             device_id=(group, device), device_id_type=MESH_IDS,
         ).start()
+
+    def wait_hands(sems, i, count):
+        many = r_all.at[pl.ds(0, r_cols), pl.ds(0, count * rows)]
+        pltpu.make_async_copy(many, many, sems.at[i]).wait()
+
+    hand(r_part, r_all.at[r_rows, home], 0, far[0])
+    for device in near:
+        hand(r_part, r_all.at[r_rows, home], 1, device)
 
     def step(e, carry):
         merge(0, e)
         start_sends(1, e - 1)
-        after_first(e)
+        merge(1, e)
+        start_sends(0, e)
         return carry
 
     lax.fori_loop(1, experts, step, 0)
 
-    many = r_all.at[pl.ds(0, r_cols), pl.ds(0, (n - 1) * rows)]
-    pltpu.make_async_copy(many, many, r_recv).wait()
-    pltpu.make_async_copy(many, many, r_send).wait()
+    wait_hands(r_recv, 0, 1)
+    mirror = r_all.at[r_rows, pl.ds(pl.multiple_of(far[0] * rows, rows), rows)]
+    for device in near:
+        hand(mirror, mirror, 2, device)
     start_sends(1, experts - 1)
+    wait_hands(r_send, 0, 1)
+    for i in (1, 2):
+        wait_hands(r_recv, i, len(near))
+        wait_hands(r_send, i, len(near))
     for g in other:
         pltpu.make_async_remote_copy(
             src_ref=r_all.at[r_rows, :], dst_ref=r_all.at[r_rows, :], send_sem=f_send, recv_sem=f_recv,
@@ -177,11 +189,17 @@
     lax.fori_loop(0, experts, arrive, 0)
 
 
-def put_kernel(gate, up, router, og, ou, orr, done):
+PIECES = 4
+
+
+def put_kernel(gate, up, router, og, ou, orr, done, done_router):
+    size = gate.shape[0] // PIECES
     copies = [
-        pltpu.make_async_copy(src, dst, done.at[i])
-        for i, (src, dst) in enumerate(((gate, og), (up, ou), (router, orr)))
+        pltpu.make_async_copy(src.at[pl.ds(i * size, size)], dst.at[pl.ds(i * size, size)], done.at[a, i])
+        for i in range(PIECES)
+        for a, (src, dst) in enumerate(((gate, og), (up, ou)))
     ]
+    copies.append(pltpu.make_async_copy(router, orr, done_router))
     for copy in copies:
         copy.start()
     for copy in copies:
@@ -195,7 +213,7 @@
         out_shape=tuple(pltpu.HBM(x.shape, x.dtype) for x in held),
         in_specs=[anywhere] * len(held),
         out_specs=(anywhere,) * len(held),
-        scratch_shapes=[pltpu.SemaphoreType.DMA((len(held),))],
+        scratch_shapes=[pltpu.SemaphoreType.DMA((2, PIECES)), pltpu.SemaphoreType.DMA],
         compiler_params=pltpu.CompilerParams(vmem_limit_bytes=1024 * 1024),
         name="put",
     )(*held)
@@ -226,13 +244,17 @@
             pltpu.VMEM((r_cols * groups, rows * n), jnp.bfloat16),
             dma((2, LOADS)), dma((2, LOADS)), dma((2,)),
             dma((2, SLOTS)), dma((2, SLOTS)), dma((2, experts)),
-            dma, dma, dma, dma,
+            dma((3,)), dma((3,)), dma, dma,
         ],
         compiler_params=pltpu.CompilerParams(
             collective_id=0, has_side_effects=True, vmem_limit_bytes=24 * 1024 * 1024,
         ),
         name="regroup",
-    )(master_gate, second_gate, master_up, second_up, router_weight.T, router_gain[None, :]))
+    )(
+        master_gate, second_gate, master_up, second_up,
+        pltpu.with_memory_space_constraint(router_weight.T, pltpu.HBM),
+        pltpu.with_memory_space_constraint(router_gain[None, :], pltpu.HBM),
+    ))
 
 
 def solution(mesh):
@@ -242,8 +264,8 @@
         experts, rows, inner = args[0].shape
         r_cols = args[4].shape[1]
         fits = (
-            n % 2 == 0 and groups > 1 and rows % 128 == 0 and inner % 128 == 0
-            and (inner // n) % 16 == 0 and r_cols % 16 == 0 and experts >= max(SLOTS, LOADS)
+            n % 2 == 0 and n > 2 and groups > 1 and rows % 128 == 0 and inner % 128 == 0
+            and (inner // n) % 16 == 0 and r_cols % 16 == 0 and experts % PIECES == 0 and experts >= max(SLOTS, LOADS)
         )
         return fused(n, groups, *args) if fits else plain(*args)
 

time: 562 us -> 558 us (level)
  no operation moved by 1% of the time
where the time goes in v2:
time: 558 us
  Pallas kernels  557 us (100%)
    pallas_call x1, Pallas kernels, fused(): pl.pallas_call(functools.partial(regroup_kernel, n, groups), out_shape=(p...  549 us

profile of v2, /device:TPU:0, one launch (start us, length us, event | category | flops | bytes accessed | tf_op | source)
XLA Modules:
  0.0 558.0 jit_solution(17747065503130065202)
XLA Ops:
  0.6 548.8 %regroup.1 = (bf16[32,96,2048]{2,1,0:T(8,128)(2,1)S(1)}, bf16[32,96,2048]{2,1,0:T(8,128)(2,1)S(1)}, bf16[2048,128]{1,0:T(8,128)(2,1)S(1)}) custom-call(f32[32,256,768]{2,1,0:T(8,128)} %mg.1, bf16[32,256,768]{2,1,0:T(8,128)(2,1)} %sg.1, f32[32,256,768]{2,1,0:T(8,128)} %mu.1, bf16[32,256,768]{2,1,0:T(8,128)(2,1)} %su.1, f32[32,256]{1,0:T(8,128)} %bitcast.2, ...), custom_call_target="tpu_custom_call" | custom-call | tf_op jit(solution)/shard_map/regroup/pallas_call | solution.py:228
  549.4 8.6 %put.1 = (bf16[32,96,2048]{2,1,0:T(8,128)(2,1)}, bf16[32,96,2048]{2,1,0:T(8,128)(2,1)}, bf16[2048,128]{1,0:T(8,128)(2,1)}) custom-call(bf16[32,96,2048]{2,1,0:T(8,128)(2,1)S(1)} %get-tuple-element.6.gate, bf16[32,96,2048]{2,1,0:T(8,128)(2,1)S(1)} %get-tuple-element.7.up, bf16[2048,128]{1,0:T(8,128)(2,1)S(1)} %get-tuple-element.8.router), custom_call_target="tpu_custom_call" | custom-call | tf_op jit(solution)/shard_map/put/pallas_call | solution.py:211
